TPU v7x, 256 devices: a whole 4x4x8 slice. The times are simulated.
256 devices in a mesh: row: 16 (over x, y), col: 8 (over z), depth: 2 (over core).
Axes of the slice: x: 4, y: 4, z: 8, core: 2. Of those that a mesh axis runs over, the one named last changes fastest.
Arguments:
- halves: bfloat16 [2, 8192, 16384], P(None, 'row', ('col', 'depth')), may hold values from -6 to 6
- spectrum: float32 [2, 16384], P(None, ('col', 'depth')), as said below
- wanted: int32 [4096], P('col'), may hold values from 0 to 32766, as said below
- fraction: float32 [4096], P('col'), may hold values from 0.05 to 0.95
Outputs:
- eigvec: float32 [2, 8192, 4096], P(None, 'row', ('col', 'depth'))
Inputs may be any that keep to these rules, and one draw needn't show every extreme that they name: Read in the order spectrum[0,0], spectrum[1,0], spectrum[0,1], spectrum[1,1], ... the values rise strictly, each by more than 0.05 over the one before. `wanted`: distinct positions in that merged order of the 32768 eigenvalues.
All inputs are finite; a program needn't handle non-finite values.
Results may differ from a plain program's by a relative error of at most 0.0029.
Values may be sent and summed in bfloat16 or wider, within the bound.
A program may use at most 128 MiB of HBM per device.

v0:
```python
import functools
import math

import jax
import jax.numpy as jnp
from jax import lax
from jax.sharding import Mesh
from jax.sharding import PartitionSpec as P

ROW = ("row_0", "row_1")


def over_axes(shard, axes):
    return functools.reduce(lax.psum, axes, shard)


def in_one_piece(arrays, axis, dim, along):
    both = jnp.concatenate(arrays, axis=along)
    out, at, done = (lax.all_gather(both, axis, axis=dim, tiled=True), 0, [])
    for a in arrays:
        done.append(lax.slice_in_dim(out, at, at + a.shape[along], axis=along))
        at += a.shape[along]
    return tuple(done)


def cut_along(shard, dim, size):
    shape = shard.shape
    pieces = shard.reshape(*shape[:dim], size, shape[dim] // size, *shape[dim + 1 :])
    return jnp.moveaxis(pieces, dim, 0)


def summed_on_arrival(shard, axis, dim):
    pieces = cut_along(shard, dim, lax.axis_size(axis))
    arrived = lax.all_to_all(pieces, axis, split_axis=0, concat_axis=0, tiled=True)
    return arrived.sum(axis=0)


def root_terms(spectrum_full, wanted):
    ordered = jnp.stack([spectrum_full[0], spectrum_full[1]], axis=1).reshape(-1)
    lower = jnp.take(ordered, wanted)
    upper = jnp.take(ordered, wanted + 1)
    return (lower, upper - lower)


def cauchy_block(seam_part, value_part, lower, width, frac):
    return seam_part[:, :, None] / (
        value_part[:, :, None] - lower[None, None, :] - frac[None, None, :] * width[None, None, :]
    )


def column_norms(seam_full, value_full, lower, width, frac):
    step = seam_full.shape[1] // 8
    total = jnp.zeros(lower.shape, jnp.float32)
    for part in range(8):
        cauchy = cauchy_block(
            seam_full[:, part * step : (part + 1) * step],
            value_full[:, part * step : (part + 1) * step],
            lower,
            width,
            frac,
        )
        total = total + jnp.sum(cauchy * cauchy, axis=(0, 1))
    return jnp.sqrt(total)


def panel_product(piece, seam_part, value_part, lower, width, frac):
    columns = lower.shape[0]
    block = math.gcd(columns, 128)

    def one(index):
        start = index * block
        low = lax.dynamic_slice_in_dim(lower, start, block)
        wid = lax.dynamic_slice_in_dim(width, start, block)
        frc = lax.dynamic_slice_in_dim(frac, start, block)
        cauchy = cauchy_block(seam_part, value_part, low, wid, frc)
        product = jnp.einsum(
            "arh,ahk->ark", piece, cauchy.astype(jnp.bfloat16), preferred_element_type=jnp.float32
        )
        return (product, jnp.zeros((block,), jnp.float32))

    products, sums = lax.map(one, jnp.arange(columns // block))
    product = jnp.transpose(products, (1, 2, 0, 3)).reshape(piece.shape[0], piece.shape[1], columns)
    return (product, sums.reshape(-1))


def body(halves, spectrum, wanted, fraction):
    rows_here = halves.shape[1]
    shard_width = halves.shape[2]
    place = lax.axis_index(ROW)
    low_row = jnp.where(
        place == lax.axis_size(ROW) - 1, halves[0, rows_here - 1].astype(jnp.float32), 0.0
    )
    high_row = jnp.where(place == 0, halves[1, 0].astype(jnp.float32), 0.0)
    seam = over_axes(jnp.stack([low_row, high_row]), ROW)
    seam_full, value_full = in_one_piece((seam, spectrum), ("col", "depth"), 1, 0)
    lower_col, width_col = root_terms(value_full, wanted)
    ncols = lax.axis_size("col")
    ndepth = lax.axis_size("depth")
    layer = lax.axis_index("depth")
    seam_mine = lax.dynamic_index_in_dim(
        seam_full.reshape(2, ncols, ndepth, shard_width), layer, 2, keepdims=False
    ).reshape(2, ncols * shard_width)
    value_mine = lax.dynamic_index_in_dim(
        value_full.reshape(2, ncols, ndepth, shard_width), layer, 2, keepdims=False
    ).reshape(2, ncols * shard_width)
    share = lower_col.shape[0] // ndepth
    product, sums = panel_product(
        lax.all_gather(halves, "col", axis=2, tiled=True),
        seam_mine,
        value_mine,
        lower_col,
        width_col,
        fraction,
    )
    total = product
    product = summed_on_arrival(total, "depth", 2)
    lower_own = lax.dynamic_slice_in_dim(lower_col, layer * share, share)
    width_own = lax.dynamic_slice_in_dim(width_col, layer * share, share)
    frac_own = lax.dynamic_slice_in_dim(fraction, layer * share, share)
    norms = column_norms(seam_full, value_full, lower_own, width_own, frac_own)
    return product / norms[None, None, :]


def solution(mesh):
    split = Mesh(
        mesh.devices.reshape(4, 4, mesh.shape["col"], mesh.shape["depth"]),
        ("row_0", "row_1", "col", "depth"),
    )
    in_specs = (P(None, ROW, ("col", "depth")), P(None, ("col", "depth")), P("col"), P("col"))
    out_specs = P(None, ROW, ("col", "depth"))
    return jax.shard_map(body, mesh=split, in_specs=in_specs, out_specs=out_specs, check_vma=False)
```

profile of v0, /device:TPU:1, one launch (start us, length us, event | category | flops | bytes accessed | tf_op | source)
XLA Modules:
  0.0 244.6 jit_solution(11194111778540224851)
XLA Ops:
  6.5 0.7 all-gather.2.cloned.1.call-update
  7.3 0.7 fusion.7
  8.1 9.4 %psum.14 = f32[2,1024]{1,0:T(2,128)S(1)} all-reduce(f32[2,1024]{1,0:T(2,128)S(1)} %pad_maximum_fusion.2), channel_id=1, replica_groups=mesh['row_0'=4,'row_1'=4,'col'=8,'depth'=2] {'row_0'}, use_global_device_ids=true, to_apply=%region_0.1 | all-reduce | flops 2048 | bytes 16384 | tf_op jit(solution)/shard_map/psum | solution.py:14
  17.5 9.0 %psum.15 = f32[2,1024]{1,0:T(2,128)S(1)} all-reduce(f32[2,1024]{1,0:T(2,128)S(1)} %psum.14), channel_id=1, replica_groups=mesh['row_0'=4,'row_1'=4,'col'=8,'depth'=2] {'row_1'}, use_global_device_ids=true, to_apply=%region_1.2 | all-reduce | flops 2048 | bytes 16384 | tf_op jit(solution)/shard_map/psum | solution.py:14
  26.5 0.7 pad_maximum_fusion.1
  27.2 26.9 %all_gather.6 = f32[4,16384]{1,0:T(4,128)S(1)} all-gather(f32[4,1024]{1,0:T(4,128)S(1)} %pad_maximum_fusion.1), channel_id=1, replica_groups=mesh['row_0'=4,'row_1'=4,'col'=8,'depth'=2] {'col','depth'}, dimensions={1}, use_global_device_ids=true | all-gather | bytes 278528 | tf_op jit(solution)/shard_map/all_gather | solution.py:19
  54.1 0.1 slice_bitcast_fusion.1
  54.3 0.1 pad_maximum_fusion
  54.4 5.0 %copy.20 = f32[16384,2]{1,0:T(8,128)} copy(f32[16384,2]{0,1:T(2,128)S(1)} %pad_maximum_fusion) | data formatting | bytes 262144 | tf_op jit(solution)/shard_map/stack | solution.py:39
  59.3 7.0 %reshape.100 = f32[32768]{0:T(1024)S(1)} reshape(f32[16384,2]{1,0:T(8,128)} %copy.20) | data formatting | bytes 262144 | tf_op jit(solution)/shard_map/reshape | solution.py:39
  66.4 3.1 %gather_fusion = f32[512]{0:T(512)S(1)} fusion(f32[32768]{0:T(1024)S(1)} %reshape.100, s32[1024]{0:T(1024)S(1)} %get-tuple-element.109), kind=kCustom, calls=%fused_computation.clone | custom fusion | bytes 6144 | tf_op jit(solution)/shard_map/jit(_take)/gather | solution.py:40
  69.5 3.1 %gather_fusion.1 = f32[512]{0:T(512)S(1)} fusion(f32[32768]{0:T(1024)S(1)} %reshape.100, s32[1024]{0:T(1024)S(1)} %get-tuple-element.108), kind=kCustom, calls=%fused_computation.1.clone | custom fusion | bytes 6144 | tf_op jit(solution)/shard_map/jit(_take)/gather | solution.py:41
  72.7 0.1 fusion.10
  72.8 0.2 reshape.98
  73.0 0.2 reshape.99
  73.1 0.1 constant_dynamic-slice_fusion
  73.4 0.1 dynamic_slice.31
  73.4 0.1 dynamic-slice_multiply_fusion.1
  73.5 0.1 fusion.9
  73.6 9.4 %multiply_reduce_fusion.6 = (f32[256]{0:T(256)S(1)}, f32[256]{0:T(256)S(1)}, f32[256]{0:T(256)S(1)}, f32[256]{0:T(256)S(1)}, f32[256]{0:T(256)S(1)}, /*index=5*/f32[256]{0:T(256)S(1)}, f32[256]{0:T(256)S(1)}, f32[256]{0:T(256)S(1)}) fusion(f32[2,2048]{1,0:T(2,128)S(1)} %get-tuple-element.97, f32[2,2048]{1,0:T(2,128)S(1)} %get-tuple-element.98, ...), kind=kLoop, calls=%fused_computation.17 | loop fusion | flops 41940992 | bytes 272384 | tf_op jit(solution)/shard_map/reduce_sum | solution.py:62
  83.0 0.6 add_sqrt_fusion
  83.6 103.3 %all-gather.2.cloned.1.call-done = bf16[2,512,8192]{2,1,0:T(8,128)(2,1)} async-done(((bf16[2,512,1024]{2,1,0:T(8,128)(2,1)}), bf16[2,512,8192]{2,1,0:T(8,128)(2,1)}) %all-gather.2.cloned.1.call-update) | async-done | bytes 16777232 | tf_op jit(solution)/shard_map/all_gather | solution.py:108
  186.9 43.0 %while.10 = (s32[]{:T(128)}, f32[4,2,512,128]{2,3,0,1:T(8,128)S(1)}, f32[2,8,1024]{2,1,0:T(8,128)S(1)}, f32[2,8,1024]{2,1,0:T(8,128)S(1)}, s32[4]{0:T(128)S(1)},...) while((s32[]{:T(128)}, ...), condition=%wide.region_3.5_spmd, body=%wide.region_2.4_spmd.sunk | while | flops 2155872512 | bytes 17698500 | solution.py:81
  186.9 0.6 dynamic_slice.46
  188.1 0.1 dynamic-slice_multiply_fusion.3
  188.1 0.1 dynamic_slice.47
  188.3 0.1 copy.48
  188.3 9.3 %fusion.15 = f32[4,2,512,128]{2,3,0,1:T(8,128)S(1)} fusion(f32[4,2,512,128]{2,3,0,1:T(8,128)S(1)} %get-tuple-element.179, s32[]{:T(128)} %get-tuple-element.178, bf16[2,512,8192]{2,1,0:T(8,128)(2,1)} %get-tuple-element.199, f32[128]{0:T(128)S(1)} %dynamic-slice_multiply_fusion.3, f32[128]{0:T(128)S(1)} %dynamic_slice.47, f32[2,8192]{1,0:T(2,128)S(1)} %bitcast.52, ...), kind=kOutput, calls=%fused_computation.9.clone.1 | convolution fusion | flops 2155872256 | bytes 17433604 | tf_op jit(solution)/shard_map/while/body/eval_jaxpr/arh,ahk->ark/dot_general | solution.py:76
  197.7 0.6 dynamic_slice.46
  198.8 0.1 dynamic-slice_multiply_fusion.3
  198.9 0.1 dynamic_slice.47
  199.0 0.1 copy.48
  199.1 9.3 %fusion.15 = f32[4,2,512,128]{2,3,0,1:T(8,128)S(1)} fusion(f32[4,2,512,128]{2,3,0,1:T(8,128)S(1)} %get-tuple-element.179, s32[]{:T(128)} %get-tuple-element.178, bf16[2,512,8192]{2,1,0:T(8,128)(2,1)} %get-tuple-element.199, f32[128]{0:T(128)S(1)} %dynamic-slice_multiply_fusion.3, f32[128]{0:T(128)S(1)} %dynamic_slice.47, f32[2,8192]{1,0:T(2,128)S(1)} %bitcast.52, ...), kind=kOutput, calls=%fused_computation.9.clone.1 | convolution fusion | flops 2155872256 | bytes 17433604 | tf_op jit(solution)/shard_map/while/body/eval_jaxpr/arh,ahk->ark/dot_general | solution.py:76
  208.4 0.6 dynamic_slice.46
  209.6 0.1 dynamic-slice_multiply_fusion.3
  209.6 0.1 dynamic_slice.47
  209.8 0.1 copy.48
  209.8 9.3 %fusion.15 = f32[4,2,512,128]{2,3,0,1:T(8,128)S(1)} fusion(f32[4,2,512,128]{2,3,0,1:T(8,128)S(1)} %get-tuple-element.179, s32[]{:T(128)} %get-tuple-element.178, bf16[2,512,8192]{2,1,0:T(8,128)(2,1)} %get-tuple-element.199, f32[128]{0:T(128)S(1)} %dynamic-slice_multiply_fusion.3, f32[128]{0:T(128)S(1)} %dynamic_slice.47, f32[2,8192]{1,0:T(2,128)S(1)} %bitcast.52, ...), kind=kOutput, calls=%fused_computation.9.clone.1 | convolution fusion | flops 2155872256 | bytes 17433604 | tf_op jit(solution)/shard_map/while/body/eval_jaxpr/arh,ahk->ark/dot_general | solution.py:76
  219.2 0.6 dynamic_slice.46
  220.3 0.1 dynamic-slice_multiply_fusion.3
  220.4 0.1 dynamic_slice.47
  220.5 0.1 copy.48
  220.6 9.3 %fusion.15 = f32[4,2,512,128]{2,3,0,1:T(8,128)S(1)} fusion(f32[4,2,512,128]{2,3,0,1:T(8,128)S(1)} %get-tuple-element.179, s32[]{:T(128)} %get-tuple-element.178, bf16[2,512,8192]{2,1,0:T(8,128)(2,1)} %get-tuple-element.199, f32[128]{0:T(128)S(1)} %dynamic-slice_multiply_fusion.3, f32[128]{0:T(128)S(1)} %dynamic_slice.47, f32[2,8192]{1,0:T(2,128)S(1)} %bitcast.52, ...), kind=kOutput, calls=%fused_computation.9.clone.1 | convolution fusion | flops 2155872256 | bytes 17433604 | tf_op jit(solution)/shard_map/while/body/eval_jaxpr/arh,ahk->ark/dot_general | solution.py:76
  229.9 0.2 copy.22
  230.1 5.9 %all_to_all.5 = f32[2,2,512,256]{2,3,1,0:T(8,128)S(1)} all-to-all(f32[2,2,512,256]{2,3,1,0:T(8,128)S(1)} %copy.22), channel_id=1, replica_groups=mesh['row_0'=4,'row_1'=4,'col'=8,'depth'=2] {'depth'}, dimensions={0} | all-to-all | bytes 4194304 | tf_op jit(solution)/shard_map/all_to_all | solution.py:34
  236.0 0.3 reduce_sum.81
  236.3 0.1 broadcast_divide_fusion
  236.5 1.3 copy.24
  (19 shorter events, 0.3 us)
Async XLA Ops:
  6.5 180.4 %all-gather.2.cloned.1.call-start = ((), (), s32[]{:S(2)}) async-start(), calls=%async_computation.1 | async-start | bytes 18874368 | tf_op jit(solution)/shard_map/all_gather | solution.py:108
  59.3 7.0 %copy-start = (s32[512]{0:T(512)S(1)}, s32[512]{0:T(512)}, u32[]{:S(2)}) copy-start(s32[512]{0:T(512)} %param.10) | copy-start | bytes 6148
  66.4 7.1 %copy-start.1 = (f32[512]{0:T(512)S(1)}, f32[512]{0:T(512)}, u32[]{:S(2)}) copy-start(f32[512]{0:T(512)} %param.11) | copy-start | bytes 6148
  230.1 6.2 %copy-start.2 = (f32[256]{0:T(256)S(1)}, f32[256]{0:T(256)}, u32[]{:S(2)}) copy-start(f32[256]{0:T(256)} %add_sqrt_fusion) | copy-start | bytes 3076
Sparse Core Ops, SparseCore 0:
  9.1 177.7 all-gather.1
where the time goes:
time: 245 us
  waiting for transfers between devices  104 us (42%)
  blocking collectives  51.2 us (21%)
  matrix products  37.2 us (15%)
  local copies, waits for them, and re-layouts  23.7 us (10%)
  between operations  13.6 us (6%)
  other arithmetic  12.4 us (5%)
    all_gather x1, waiting for transfers between devices, body(): lax.all_gather(halves, 'col', axis=2, tiled=True)  103 us
    dot_general x4, matrix products, one(): jnp.einsum('arh,ahk->ark', piece, cauchy.astype(jnp.bfloat16), preferred_...  37.2 us
    all_gather x1, blocking collectives, in_one_piece(): out, at, done = (lax.all_gather(both, axis, axis=dim, tiled=True), 0, [])  26.9 us
    psum x2, blocking collectives, over_axes(): return functools.reduce(lax.psum, axes, shard)  18.4 us
    reduce_sum x1, other arithmetic, column_norms(): total = total + jnp.sum(cauchy * cauchy, axis=(0, 1))  9.38 us
    reshape x1, local copies, waits for them, and re-layouts, root_terms(): jnp.stack([spectrum_full[0], spectrum_full[1]], axis=1).reshape(-1)  6.99 us
    all_to_all x1, blocking collectives, summed_on_arrival(): lax.all_to_all(pieces, axis, split_axis=0, concat_axis=0, tiled=True)  5.89 us
    another operation x2, local copies, waits for them, and re-layouts, root_terms(): jnp.stack([spectrum_full[0], spectrum_full[1]], axis=1).reshape(-1)  5.07 us
  transfers between devices with their start and end apart: 1, of which 1 were waited for; matrix products, arithmetic and copies ran while one was open for 13% of the time, Pallas kernels for 0%

commit v1 on v0

v1 whole, which is shorter than its diff:
```python
import functools

import jax
import jax.numpy as jnp
from jax import lax
from jax.experimental import pallas as pl
from jax.experimental.pallas import tpu as pltpu
from jax.sharding import PartitionSpec as P

MESH = pl.DeviceIdType.MESH
LANES = 128


def log2(x):
    return x.bit_length() - 1


def kernel(
    nrow,
    n,
    halves,
    pay,
    out,
    afull,
    tab,
    seam,
    tcat,
    ct,
    part,
    sbuf,
    rbuf,
    ssq,
    ssq_s,
    ssq_r,
    lowb,
    fwb,
    a_sem,
    tab_send,
    tab_recv,
    seam_send,
    seam_recv,
    ring_send,
    ring_recv,
    ssq_send,
    ssq_recv,
):
    row, z, c = lax.axis_index("row"), lax.axis_index("col"), lax.axis_index("depth")
    rows, width = halves.shape[1], halves.shape[2]
    tiles = width // LANES
    cols = out.shape[2]
    kblocks = cols // LANES
    half = rows // 2
    me = z * 2 + c
    other = 1 - c
    first, last = row == 0, row == nrow - 1
    edge = jnp.logical_or(first, last)

    def copy_out(src, dst, send, recv, where):
        return pltpu.make_async_remote_copy(
            src_ref=src, dst_ref=dst, send_sem=send, recv_sem=recv, device_id=where, device_id_type=MESH
        )

    a_local = pltpu.make_async_copy(halves, afull.at[c], a_sem.at[0])
    a_local.start()
    tab_local = pltpu.make_async_copy(pay.at[pl.ds(2, 3)], tab.at[me], tab_recv.at[me])
    tab_local.start()

    barrier = pltpu.get_barrier_semaphore()

    def greet(where):
        pl.semaphore_signal(barrier, inc=1, device_id=where, device_id_type=MESH)

    for o in range(1, n):
        zz = lax.rem(z + o, n)
        greet((row, zz, c))
        greet((row, zz, other))
    greet((row, z, other))

    @pl.when(edge)
    def _():
        def one(i, carry):
            rr = lax.rem(row + i, nrow)
            greet((rr, z, c))
            greet((rr, z, other))
            return carry

        lax.fori_loop(1, nrow, one, 0)

    @pl.when(jnp.logical_not(edge))
    def _():
        for rr in (0, nrow - 1):
            greet((rr, z, c))
            greet((rr, z, other))

    pl.semaphore_wait(barrier, 2 * n - 1 + jnp.where(edge, 2 * (nrow - 1), 4))

    def tab_same(o):
        return copy_out(
            pay.at[pl.ds(2, 3)], tab.at[me], tab_send.at[o], tab_recv.at[me], (row, lax.rem(z + o, n), c)
        )

    def tab_other(o):
        return copy_out(
            pay.at[pl.ds(2, 2)],
            tab.at[me, pl.ds(0, 2)],
            tab_send.at[n + o],
            tab_recv.at[me],
            (row, lax.rem(z + o, n), other),
        )

    order = sorted(range(1, n), key=lambda o: -min(o, n - o))
    for o in order:
        tab_same(o).start()
        tab_other(o).start()
    tab_other(0).start()

    def seam_copy(a, i, where_c):
        return copy_out(
            pay.at[a],
            seam.at[c, a],
            seam_send.at[2 * i + where_c],
            seam_recv.at[c, a],
            (lax.rem(row + i, nrow), z, where_c),
        )

    def seam_sends(a, act):
        def one(i, carry):
            act(seam_copy(a, i, 0))
            act(seam_copy(a, i, 1))
            return carry

        lax.fori_loop(1, nrow, one, 0)
        act(copy_out(pay.at[a], seam.at[c, a], seam_send.at[0], seam_recv.at[c, a], (row, z, other)))

    for flag, a in ((last, 0), (first, 1)):

        @pl.when(flag)
        def _(a=a):
            pltpu.make_async_copy(pay.at[a], seam.at[c, a], seam_recv.at[c, a]).start()
            seam_sends(a, lambda d: d.start())

    a_swap = copy_out(halves, afull.at[c], a_sem.at[1], a_sem.at[2], (row, z, other))
    a_swap.start()

    for o in range(n):
        zz = lax.rem(z + o, n)
        g = zz * 2 + c
        pltpu.make_async_copy(tab.at[g], tab.at[g], tab_recv.at[g]).wait()
        g = zz * 2 + other
        pltpu.make_async_copy(tab.at[g, pl.ds(0, 2)], tab.at[g, pl.ds(0, 2)], tab_recv.at[g]).wait()

    table = tab[:, 0:2].reshape(2 * n * 2 * tiles, LANES) * 0.25
    hi = table.astype(jnp.bfloat16)
    rest = table - hi.astype(jnp.float32)
    mid = rest.astype(jnp.bfloat16)
    low = (rest - mid.astype(jnp.float32)).astype(jnp.bfloat16)
    tcat[:, 0:LANES] = hi
    tcat[:, LANES : 2 * LANES] = mid
    tcat[:, 2 * LANES : 3 * LANES] = low

    def pick(position):
        h = lax.shift_right_logical(position, 1)
        a = position & 1
        g = lax.shift_right_logical(h, log2(width))
        s = lax.shift_right_logical(h, log2(LANES)) & (tiles - 1)
        entry = (g * 2 + a) * tiles + s
        lane = h & (LANES - 1)
        table_rows = tcat.shape[0]
        hit = lax.broadcasted_iota(jnp.int32, (cols, table_rows), 1) == entry
        onehot = jnp.where(hit, 1.0, 0.0).astype(jnp.bfloat16)
        found = jnp.dot(onehot, tcat[...], preferred_element_type=jnp.float32)
        value = (found[:, 0:LANES] + found[:, LANES : 2 * LANES]) + found[:, 2 * LANES : 3 * LANES]
        here = lax.broadcasted_iota(jnp.int32, (cols, LANES), 1) == lane
        return jnp.sum(jnp.where(here, value, 0.0), axis=1, keepdims=True) * 4.0

    def roots(d):
        wf = tab[d * 2 + c, 2].T
        need = 2 * kblocks

        def column(at):
            got = [
                jnp.where(c == 0, wf[:, at + b : at + b + 1], wf[:, at + kblocks + b : at + kblocks + b + 1])
                for b in range(kblocks)
            ]
            return jnp.concatenate(got, axis=0)

        position = column(0).astype(jnp.int32)
        frac = column(need)
        lower = pick(position)
        upper = pick(position + 1)
        lowb[...] = jnp.broadcast_to(lower, lowb.shape)
        fwb[...] = jnp.broadcast_to(frac * (upper - lower), fwb.shape)

    def at_offset(off):
        return lax.rem(z + off + n, n)

    def ssq_copy(off):
        d = at_offset(off)
        return copy_out(
            ssq_s.at[off % n], ssq_r.at[z], ssq_send.at[off % n], ssq_recv.at[z], (row, d, c)
        )

    def cauchy(a):
        def one(t, carry):
            dp, s = t // tiles, lax.rem(t, tiles)
            value = tab[z * 2 + dp, a, pl.ds(s, 1), :]
            weight = seam[dp, a, pl.ds(s, 1), :]
            term = weight / ((value - lowb[...]) - fwb[...])
            ssq[...] += term * term
            ct[:, pl.ds(pl.multiple_of(t * LANES, LANES), LANES)] = term.astype(jnp.bfloat16)
            return carry

        lax.fori_loop(0, 2 * tiles, one, 0)

    def product(slot, a):
        dims = (((1,), (1,)), ((), ()))
        part[slot, a] = lax.dot_general(
            afull[0, a], ct[:, 0:width], dims, preferred_element_type=jnp.float32
        ) + lax.dot_general(afull[1, a], ct[:, width : 2 * width], dims, preferred_element_type=jnp.float32)

    def compute(off):
        roots(at_offset(off))
        ssq[...] = jnp.zeros_like(ssq)

        def one(a, carry):
            cauchy(a)
            product(off % n, a)
            return carry

        lax.fori_loop(0, 2, one, 0)
        line = jnp.sum(ssq[...].T, axis=0, keepdims=True)
        for b in range(kblocks):
            ssq_s[off % n, b : b + 1, :] = line[:, b * LANES : (b + 1) * LANES]

    steps = n - 1

    def ring_copy(j, way, a):
        step = 1 if way == 0 else n - 1
        return copy_out(
            sbuf.at[j, way, a],
            rbuf.at[j, way, a],
            ring_send.at[j, way, a],
            ring_recv.at[j, way, a],
            (row, lax.rem(z + step, n), c),
        )

    def offset_of(j, way):
        off = n // 2 - (j + 1) // 2
        return off if way == 0 else -off

    def half_of(j, way):
        return (j + way) % 2

    def mine(j, way, a):
        off, hh = offset_of(j, way), half_of(j, way)
        return part[off % n, a, hh * half : (hh + 1) * half, :]

    def launch(j, way):
        for a in range(2):
            sbuf[j, way, a] = mine(j, way, a).astype(jnp.bfloat16)
            ring_copy(j, way, a).start()

    def relay(j):
        for a in range(2):
            for way in range(2):
                ring_copy(j - 2, way, a).wait_recv()
                total = mine(j, way, a) + rbuf[j - 2, way, a].astype(jnp.float32)
                sbuf[j, way, a] = total.astype(jnp.bfloat16)
                ring_copy(j, way, a).start()

    for cc in range(2):
        for a in range(2):
            pltpu.make_async_copy(seam.at[cc, a], seam.at[cc, a], seam_recv.at[cc, a]).wait()
    a_local.wait()
    a_swap.wait_recv()

    m = n // 2
    plan = [m]
    for off in range(m - 1, 0, -1):
        plan += [off, -off]
    plan.append(0)
    done_relay = 2
    for i, off in enumerate(plan):
        compute(off)
        if off != 0:
            ssq_copy(off).start()
        if i == 0:
            launch(0, 0)
            launch(0, 1)
        elif i == 1:
            launch(1, 0)
        elif i == 2:
            launch(1, 1)
        elif i >= 4 and i % 2 == 0 and done_relay < steps:
            relay(done_relay)
            done_relay += 1
    for j in range(done_relay, steps):
        relay(j)

    total = ssq_s[0]
    for o in range(1, n):
        zz = lax.rem(z + o, n)
        pltpu.make_async_copy(ssq_r.at[zz], ssq_r.at[zz], ssq_recv.at[zz]).wait()
        total = total + ssq_r[zz]
    norm = jnp.sqrt(total)
    norm = jnp.concatenate([norm[b : b + 1] for b in range(kblocks)], axis=1)
    for hh in range(2):
        for a in range(2):
            value = part[0, a, hh * half : (hh + 1) * half, :]
            for way in range(2):
                j = steps - 2 + (hh + way + steps) % 2
                ring_copy(j, way, a).wait_recv()
                value = value + rbuf[j, way, a].astype(jnp.float32)
            out[a, hh * half : (hh + 1) * half, :] = value / norm

    for o in order:
        tab_same(o).wait_send()
        tab_other(o).wait_send()
    tab_other(0).wait_send()
    for flag, a in ((last, 0), (first, 1)):

        @pl.when(flag)
        def _(a=a):
            seam_sends(a, lambda d: d.wait_send())

    a_swap.wait_send()
    for off in plan[:-1]:
        ssq_copy(off).wait_send()
    for j in range(steps):
        for way in range(2):
            for a in range(2):
                ring_copy(j, way, a).wait_send()


def merge(nrow, n, halves, spectrum, wanted, fraction):
    rows, width = halves.shape[1:]
    tiles = width // LANES
    cols = wanted.shape[0] // 2
    seam = jnp.stack([halves[0, rows - 1], halves[1, 0]]).astype(jnp.float32)
    pay = jnp.concatenate(
        [
            seam.reshape(2, tiles, LANES),
            spectrum.reshape(2, tiles, LANES),
            jnp.concatenate([wanted.astype(jnp.float32), fraction]).reshape(1, 4 * cols // LANES, LANES),
        ],
        axis=0,
    )
    half = rows // 2
    steps = n - 1
    bf16, f32 = jnp.bfloat16, jnp.float32
    return pl.pallas_call(
        functools.partial(kernel, nrow, n),
        out_shape=jax.ShapeDtypeStruct((2, rows, cols), f32),
        in_specs=[pl.BlockSpec(memory_space=pl.ANY), pl.BlockSpec(memory_space=pltpu.VMEM)],
        out_specs=pl.BlockSpec(memory_space=pltpu.VMEM),
        scratch_shapes=[
            pltpu.VMEM((2, 2, rows, width), bf16),
            pltpu.VMEM((2 * n, 3, tiles, LANES), f32),
            pltpu.VMEM((2, 2, tiles, LANES), f32),
            pltpu.VMEM((2 * n * 2 * tiles, 3 * LANES), bf16),
            pltpu.VMEM((cols, 2 * width), bf16),
            pltpu.VMEM((n, 2, rows, cols), f32),
            pltpu.VMEM((steps, 2, 2, half, cols), bf16),
            pltpu.VMEM((steps, 2, 2, half, cols), bf16),
            pltpu.VMEM((cols, LANES), f32),
            pltpu.VMEM((n, cols // LANES, LANES), f32),
            pltpu.VMEM((n, cols // LANES, LANES), f32),
            pltpu.VMEM((cols, LANES), f32),
            pltpu.VMEM((cols, LANES), f32),
            pltpu.SemaphoreType.DMA((3,)),
            pltpu.SemaphoreType.DMA((2 * n,)),
            pltpu.SemaphoreType.DMA((2 * n,)),
            pltpu.SemaphoreType.DMA((2 * nrow,)),
            pltpu.SemaphoreType.DMA((2, 2)),
            pltpu.SemaphoreType.DMA((steps, 2, 2)),
            pltpu.SemaphoreType.DMA((steps, 2, 2)),
            pltpu.SemaphoreType.DMA((n,)),
            pltpu.SemaphoreType.DMA((n,)),
        ],
        compiler_params=pltpu.CompilerParams(
            collective_id=0, has_side_effects=True, vmem_limit_bytes=48 * 1024 * 1024
        ),
        name="merge",
    )(halves, pay)


def solution(mesh):
    body = functools.partial(merge, mesh.shape["row"], mesh.shape["col"])
    in_specs = (P(None, "row", ("col", "depth")), P(None, ("col", "depth")), P("col"), P("col"))
    out_specs = P(None, "row", ("col", "depth"))
    return jax.shard_map(body, mesh=mesh, in_specs=in_specs, out_specs=out_specs, check_vma=False)
```

time: 245 us -> 76.1 us (0.31)
  waiting for transfers between devices: 104 us -> 0 us
  Pallas kernels: 0 us -> 70.3 us
  blocking collectives: 51.2 us -> 0 us
  matrix products: 37.2 us -> 0 us
  local copies, waits for them, and re-layouts: 23.7 us -> 4.03 us
  between operations: 13.6 us -> 0.02 us
  other arithmetic: 12.4 us -> 1.39 us
    all_gather x1 -> x0, waiting for transfers between devices: 103 us -> none  [body(): lax.all_gather(halves, 'col', axis=2, tiled=True)]
    pallas_call x0 -> x1, Pallas kernels: none -> 70.3 us  [merge(): pl.pallas_call(functools.partial(kernel, nrow, n), out_shape=jax.ShapeDty...]
    dot_general x4 -> x0, matrix products: 37.2 us -> none  [one(): jnp.einsum('arh,ahk->ark', piece, cauchy.astype(jnp.bfloat16), preferred_...]
    all_gather x1 -> x0, blocking collectives: 26.9 us -> none  [in_one_piece(): out, at, done = (lax.all_gather(both, axis, axis=dim, tiled=True), 0, [])]
    psum x2 -> x0, blocking collectives: 18.4 us -> none  [over_axes(): return functools.reduce(lax.psum, axes, shard)]
    reduce_sum x2 -> x0, other arithmetic: 9.68 us -> none  [the longest x1 9.38 us: column_norms(): total = total + jnp.sum(cauchy * cauchy, axis=(0, 1))]
    reshape x3 -> x0, local copies, waits for them, and re-layouts: 7.31 us -> none  [the longest x1 6.99 us: root_terms(): jnp.stack([spectrum_full[0], spectrum_full[1]], axis=1).reshape(-1)]
    gather x2 -> x0, local copies, waits for them, and re-layouts: 6.29 us -> none  [the longest x1 3.14 us: root_terms(): upper = jnp.take(ordered, wanted + 1)]
  transfers between devices with their start and end apart: 1 -> 0, of which waited for: 1 -> 0; matrix products, arithmetic and copies ran while one was open for 13% -> 0% of each run, Pallas kernels for 0% -> 0%
where the time goes in v1:
time: 76.1 us; the launch traced here: 75.7 us
  Pallas kernels  70.3 us (92%)
  local copies, waits for them, and re-layouts  4.03 us (5%)
  other arithmetic  1.39 us (2%)
    pallas_call x1, Pallas kernels, merge(): pl.pallas_call(functools.partial(kernel, nrow, n), out_shape=jax.ShapeDty...  70.3 us
    unnamed x4, local copies, waits for them, and re-layouts  3.26 us

profile of v1, /device:TPU:1, one launch (start us, length us, event | category | flops | bytes accessed | tf_op | source)
XLA Modules:
  0.0 75.7 jit_solution(3589018291391199546)
XLA Ops:
  0.0 0.7 convert_element_type.8
  0.7 0.7 maximum_bitcast_fusion
  1.4 0.8 %slice_reduce_fusion.1 = (bf16[1024]{0:T(1024)(128)(2,1)S(1)}, bf16[1024]{0:T(1024)(128)(2,1)S(1)}) fusion(bf16[2,512,1024]{2,1,0:T(8,128)(2,1)} %halves.1), kind=kLoop, calls=%fused_computation.5 | loop fusion | bytes 8192 | tf_op jit(solution)/shard_map/slice | solution.py:339
  2.2 0.7 copy.7
  2.9 0.0 copy-start
  2.9 1.6 %copy-done = bf16[2,512,1024]{2,1,0:T(8,128)(2,1)S(1)} copy-done((bf16[2,512,1024]{2,1,0:T(8,128)(2,1)S(1)}, bf16[2,512,1024]{2,1,0:T(8,128)(2,1)}, u32[]{:S(2)}) %copy-start) | copy-done | bytes 2097176
  4.5 70.3 %merge.1 = f32[2,512,256]{2,1,0:T(8,128)S(1)} custom-call(bf16[2,512,1024]{2,1,0:T(8,128)(2,1)S(1)} %copy-done, f32[5,8,128]{2,1,0:T(8,128)S(1)} %pad_maximum_fusion.pay), custom_call_target="tpu_custom_call" | custom-call | tf_op jit(solution)/shard_map/merge/pallas_call | solution.py:351
  74.7 1.0 %copy.9 = f32[2,512,256]{2,1,0:T(8,128)} copy(f32[2,512,256]{2,1,0:T(8,128)S(1)} %merge.1) | data formatting | bytes 2097152
  (2 shorter events, 0.0 us)
Async XLA Ops:
  2.9 1.6 %copy-start = (bf16[2,512,1024]{2,1,0:T(8,128)(2,1)S(1)}, bf16[2,512,1024]{2,1,0:T(8,128)(2,1)}, u32[]{:S(2)}) copy-start(bf16[2,512,1024]{2,1,0:T(8,128)(2,1)} %halves.1) | copy-start | bytes 6291460

commit v2 on v1

v2 whole, which is shorter than its diff:
```python
import functools

import jax
import jax.numpy as jnp
from jax import lax
from jax.experimental import pallas as pl
from jax.experimental.pallas import tpu as pltpu
from jax.sharding import PartitionSpec as P

MESH = pl.DeviceIdType.MESH
LANES = 128


def log2(x):
    return x.bit_length() - 1


def kernel(
    nrow,
    n,
    halves,
    spectrum,
    wanted,
    fraction,
    out,
    afull,
    edges,
    edge_row,
    tab,
    near,
    want,
    frac,
    seam,
    specb,
    seamb,
    tcat,
    ct,
    part,
    sbuf,
    rbuf,
    ssq_s,
    ssq_r,
    a_sem,
    local_sem,
    tab_sem,
    want_sem,
    frac_sem,
    seam_send,
    seam_recv,
    ring_send,
    ring_recv,
    ssq_sem,
):
    row, z, c = lax.axis_index("row"), lax.axis_index("col"), lax.axis_index("depth")
    rows, width = halves.shape[1], halves.shape[2]
    tiles = width // LANES
    cols = out.shape[2]
    kblocks = cols // LANES
    half = rows // 2
    other = 1 - c
    first, last = row == 0, row == nrow - 1
    edge = jnp.logical_or(first, last)

    def copy_out(src, dst, send, recv, where):
        return pltpu.make_async_remote_copy(
            src_ref=src, dst_ref=dst, send_sem=send, recv_sem=recv, device_id=where, device_id_type=MESH
        )

    own = pl.ds(pl.multiple_of(c * width, width), width)
    sources = [
        (spectrum.at[:, 0], tab.at[c, z, 0]),
        (spectrum.at[:, 1], tab.at[c, z, 1]),
        (wanted.at[c], want.at[z]),
        (fraction.at[c], frac.at[z]),
        (halves.at[0, pl.ds(rows - 8, 8)], edges.at[0]),
        (halves.at[1, pl.ds(0, 8)], edges.at[1]),
    ]
    local = [pltpu.make_async_copy(src, dst, local_sem.at[k]) for k, (src, dst) in enumerate(sources)]
    for d in local:
        d.start()
    a_local = pltpu.make_async_copy(halves, afull.at[:, :, own], a_sem.at[0])
    a_local.start()

    barrier = pltpu.get_barrier_semaphore()

    def greet(where):
        pl.semaphore_signal(barrier, inc=1, device_id=where, device_id_type=MESH)

    order = sorted(range(1, n), key=lambda o: -min(o, n - o))
    for o in order:
        zz = lax.rem(z + o, n)
        greet((row, zz, c))
    greet((row, z, other))

    @pl.when(edge)
    def _():
        def one(i, carry):
            rr = lax.rem(row + i, nrow)
            greet((rr, z, c))
            greet((rr, z, other))
            return carry

        lax.fori_loop(1, nrow, one, 0)

    @pl.when(jnp.logical_not(edge))
    def _():
        for rr in (0, nrow - 1):
            greet((rr, z, c))
            greet((rr, z, other))

    for d in local:
        d.wait()

    def spread(rows_of, target, a, dp):
        turned = rows_of.T
        for s in range(tiles):
            at = pl.multiple_of(dp * width + s * LANES, LANES)
            target[a, pl.ds(at, LANES), :] = jnp.broadcast_to(turned[:, s : s + 1], (LANES, LANES))

    for a in range(2):
        line = edges[a].astype(jnp.float32)
        line = line[7:8] if a == 0 else line[0:1]
        for s in range(tiles):
            edge_row[a, s : s + 1, :] = line[:, s * LANES : (s + 1) * LANES]
    for a in range(2):
        spread(tab[c, z, a], specb, a, c)

    pl.semaphore_wait(barrier, n + jnp.where(edge, 2 * (nrow - 1), 4))

    for o in order:
        where = (row, lax.rem(z + o, n), c)
        for ref, sem in ((tab.at[c, z], tab_sem), (want.at[z], want_sem), (frac.at[z], frac_sem)):
            copy_out(ref, ref, sem.at[0], sem.at[1], where).start()

    def seam_copy(a, i, where_c):
        return copy_out(
            edge_row.at[a],
            seam.at[c, a],
            seam_send,
            seam_recv.at[c, a],
            (lax.rem(row + i, nrow), z, where_c),
        )

    for flag, a in ((last, 0), (first, 1)):

        @pl.when(flag)
        def _(a=a):
            def one(i, carry):
                seam_copy(a, i, 0).start()
                seam_copy(a, i, 1).start()
                return carry

            pltpu.make_async_copy(edge_row.at[a], seam.at[c, a], seam_recv.at[c, a]).start()
            seam_copy(a, 0, other).start()
            lax.fori_loop(1, nrow, one, 0)

    near_copy = copy_out(tab.at[c, z], near, tab_sem.at[4], tab_sem.at[5], (row, z, other))
    near_copy.start()

    a_swap = [
        copy_out(halves.at[a], afull.at[a, :, own], a_sem.at[1 + a], a_sem.at[3 + a], (row, z, other))
        for a in range(2)
    ]
    for d in a_swap:
        d.start()

    def arrived(ref, sem):
        pltpu.make_async_copy(ref, ref, sem).wait()

    near_copy.wait_recv()
    for a in range(2):
        spread(near[a], specb, a, other)

    others = pl.ds(0, n - 1)
    arrived(tab.at[c, others], tab_sem.at[1])
    tab_swap = copy_out(tab.at[c], tab.at[c], tab_sem.at[2], tab_sem.at[3], (row, z, other))
    tab_swap.start()
    pairs = [(dp, a) for dp in range(2) for a in range(2)]
    for dp, a in pairs:
        arrived(seam.at[dp, a], seam_recv.at[dp, a])
    for dp, a in pairs:
        spread(seam[dp, a], seamb, a, dp)
    arrived(want.at[others], want_sem.at[1])
    arrived(frac.at[others], frac_sem.at[1])
    arrived(tab.at[other], tab_sem.at[3])

    table = (tab[...].reshape(4 * n * tiles, LANES) * 0.25).T
    hi = table.astype(jnp.bfloat16)
    rest = table - hi.astype(jnp.float32)
    mid = rest.astype(jnp.bfloat16)
    low = (rest - mid.astype(jnp.float32)).astype(jnp.bfloat16)
    tcat[0:LANES] = hi
    tcat[LANES : 2 * LANES] = mid
    tcat[2 * LANES : 3 * LANES] = low

    def pick(position):
        h = lax.shift_right_logical(position, 1)
        a = position & 1
        g = lax.shift_right_logical(h, log2(width))
        s = lax.shift_right_logical(h, log2(LANES)) & (tiles - 1)
        entry = (((g & 1) * n + lax.shift_right_logical(g, 1)) * 2 + a) * tiles + s
        lane = h & (LANES - 1)
        hit = lax.broadcasted_iota(jnp.int32, (tcat.shape[1], cols), 0) == entry
        onehot = jnp.where(hit, 1.0, 0.0).astype(jnp.bfloat16)
        found = jnp.dot(tcat[...], onehot, preferred_element_type=jnp.float32)
        value = (found[0:LANES] + found[LANES : 2 * LANES]) + found[2 * LANES : 3 * LANES]
        here = lax.broadcasted_iota(jnp.int32, (LANES, cols), 0) == lane
        return jnp.sum(jnp.where(here, value, 0.0), axis=0, keepdims=True) * 4.0

    def roots(d):
        def line(ref):
            block = ref[d]
            return jnp.concatenate([block[b : b + 1] for b in range(kblocks)], axis=1)

        position = line(want)
        lower = pick(position)
        upper = pick(position + 1)
        return lower, line(frac) * (upper - lower)

    def at_offset(off):
        return lax.rem(z + off + n, n)

    def ssq_copy(off):
        return copy_out(
            ssq_s.at[lax.rem(off + n, n)], ssq_r.at[z], ssq_sem.at[0], ssq_sem.at[1], (row, at_offset(off), c)
        )

    step_rows = 64

    def cauchy(a, lower, scaled, carry):
        def one(t, carry):
            at = pl.ds(t * step_rows, step_rows)
            value = specb[a, at, :]
            weight = seamb[a, at, :]
            sums = []
            for b in range(kblocks):
                lanes = slice(b * LANES, (b + 1) * LANES)
                term = weight / ((value - lower[:, lanes]) - scaled[:, lanes])
                ct[at, lanes] = term.astype(jnp.bfloat16)
                squares = (term * term).reshape(step_rows // 8, 8, LANES)
                sums.append(carry[b] + jnp.sum(squares, axis=0))
            return tuple(sums)

        for t in range(2 * width // step_rows):
            carry = one(t, carry)
        return carry

    def product(slot, a):
        part[slot, a] = jnp.dot(afull[a], ct[...], preferred_element_type=jnp.float32)

    steps = n - 1
    m = n // 2

    def ring_copy(j, way, a):
        step = 1 if way == 0 else n - 1
        return copy_out(
            sbuf.at[j, way, a],
            rbuf.at[j, way, a],
            ring_send.at[way, a],
            ring_recv.at[j, way, a],
            (row, lax.rem(z + step, n), c),
        )

    def mine(j, way, a):
        off = m - lax.div(j + 1, 2)
        slot = off if way == 0 else lax.rem(n - off, n)
        start = pl.multiple_of(lax.rem(j + way, 2) * half, half)
        return part[slot, a, pl.ds(start, half), :]

    def launch(j, way, a):
        sbuf[j, way, a] = mine(j, way, a).astype(jnp.bfloat16)
        ring_copy(j, way, a).start()

    def relay(j, way, a):
        ring_copy(j - 2, way, a).wait_recv()
        total = mine(j, way, a) + rbuf[j - 2, way, a].astype(jnp.float32)
        sbuf[j, way, a] = total.astype(jnp.bfloat16)
        ring_copy(j, way, a).start()

    def stage(i, carry):
        odd = lax.rem(i, 2) == 1
        off = jnp.where(odd, m - lax.div(i + 1, 2), lax.div(i, 2) - m)
        slot = lax.rem(off + n, n)
        lower, scaled = roots(at_offset(off))

        def one(a, sums):
            sums = cauchy(a, lower, scaled, sums)
            product(slot, a)
            for way in range(2):

                @pl.when(jnp.logical_or(i == 0, i == way + 1))
                def _(way=way):
                    launch(jnp.minimum(i, 1), way, a)

            return sums

        zeros = tuple(jnp.zeros((8, LANES), jnp.float32) for _ in range(kblocks))
        sums = lax.fori_loop(0, 2, one, zeros)
        for b in range(kblocks):
            ssq_s[slot, b : b + 1, :] = jnp.sum(sums[b], axis=0, keepdims=True)

        @pl.when(i >= 3)
        def _():
            def each(a, carry):
                for way in range(2):
                    relay(i - 1, way, a)
                return carry

            lax.fori_loop(0, 2, each, 0)

        @pl.when(i < n - 1)
        def _():
            ssq_copy(off).start()

        return carry

    a_local.wait()
    for d in a_swap:
        d.wait_recv()
    lax.fori_loop(0, n, stage, 0)

    for ref, sem in ((tab.at[c, others], tab_sem), (want.at[others], want_sem), (frac.at[others], frac_sem)):
        arrived(ref, sem.at[0])
    arrived(ssq_s.at[others], ssq_sem.at[0])
    tab_swap.wait_send()
    for d in a_swap:
        d.wait_send()
    near_copy.wait_send()
    for flag in (last, first):

        @pl.when(flag)
        def _():
            arrived(specb.at[0, pl.ds(0, (2 * nrow - 1) * tiles), :], seam_send)

    arrived(ssq_r.at[others], ssq_sem.at[1])
    total = ssq_s[0]
    for o in range(1, n):
        total = total + ssq_r[lax.rem(z + o, n)]
    norm = jnp.sqrt(total)
    norm = jnp.concatenate([norm[b : b + 1] for b in range(kblocks)], axis=1)
    inverse = 1.0 / norm

    def landed(j, way, a):
        ring_copy(j, way, a).wait_recv()
        hh = (j + way) % 2
        return slice(hh * half, (hh + 1) * half), rbuf[j, way, a].astype(jnp.float32)

    for a in range(2):
        for way in range(2):
            at, value = landed(steps - 2, way, a)
            part[0, a, at, :] += value
    for a in range(2):
        for way in range(2):
            at, value = landed(steps - 1, way, a)
            out[a, at, :] = (part[0, a, at, :] + value) * inverse

    for way in range(2):
        for a in range(2):
            arrived(sbuf.at[:, way, a], ring_send.at[way, a])


def merge(nrow, n, halves, spectrum, wanted, fraction):
    rows, width = halves.shape[1:]
    tiles = width // LANES
    cols = wanted.shape[0] // 2
    kblocks = cols // LANES
    spectrum = spectrum.reshape(2, tiles, LANES).transpose(1, 0, 2)
    operands = (halves, spectrum, wanted.reshape(2, kblocks, LANES), fraction.reshape(2, kblocks, LANES))
    half = rows // 2
    steps = n - 1
    bf16, f32 = jnp.bfloat16, jnp.float32
    return pl.pallas_call(
        functools.partial(kernel, nrow, n),
        out_shape=jax.ShapeDtypeStruct((2, rows, cols), f32),
        in_specs=[pl.BlockSpec(memory_space=pltpu.HBM)] * 4,
        out_specs=pl.BlockSpec(memory_space=pltpu.VMEM),
        scratch_shapes=[
            pltpu.VMEM((2, rows, 2 * width), bf16),
            pltpu.VMEM((2, 8, width), bf16),
            pltpu.VMEM((2, tiles, LANES), f32),
            pltpu.VMEM((2, n, 2, tiles, LANES), f32),
            pltpu.VMEM((2, tiles, LANES), f32),
            pltpu.VMEM((n, kblocks, LANES), jnp.int32),
            pltpu.VMEM((n, kblocks, LANES), f32),
            pltpu.VMEM((2, 2, tiles, LANES), f32),
            pltpu.VMEM((2, 2 * width, LANES), f32),
            pltpu.VMEM((2, 2 * width, LANES), f32),
            pltpu.VMEM((3 * LANES, 4 * n * tiles), bf16),
            pltpu.VMEM((2 * width, cols), bf16),
            pltpu.VMEM((n, 2, rows, cols), f32),
            pltpu.VMEM((steps, 2, 2, half, cols), bf16),
            pltpu.VMEM((steps, 2, 2, half, cols), bf16),
            pltpu.VMEM((n, kblocks, LANES), f32),
            pltpu.VMEM((n, kblocks, LANES), f32),
            pltpu.SemaphoreType.DMA((5,)),
            pltpu.SemaphoreType.DMA((6,)),
            pltpu.SemaphoreType.DMA((6,)),
            pltpu.SemaphoreType.DMA((2,)),
            pltpu.SemaphoreType.DMA((2,)),
            pltpu.SemaphoreType.DMA,
            pltpu.SemaphoreType.DMA((2, 2)),
            pltpu.SemaphoreType.DMA((2, 2)),
            pltpu.SemaphoreType.DMA((steps, 2, 2)),
            pltpu.SemaphoreType.DMA((2,)),
        ],
        compiler_params=pltpu.CompilerParams(
            collective_id=0, has_side_effects=True, vmem_limit_bytes=48 * 1024 * 1024
        ),
        name="merge",
    )(*[pltpu.with_memory_space_constraint(x, pltpu.HBM) for x in operands])


def solution(mesh):
    body = functools.partial(merge, mesh.shape["row"], mesh.shape["col"])
    in_specs = (P(None, "row", ("col", "depth")), P(None, ("col", "depth")), P("col"), P("col"))
    out_specs = P(None, "row", ("col", "depth"))
    return jax.shard_map(body, mesh=mesh, in_specs=in_specs, out_specs=out_specs, check_vma=False)
```

time: 76.1 us -> 61.2 us (0.80)
  Pallas kernels: 70.3 us -> 60.1 us
  local copies, waits for them, and re-layouts: 4.03 us -> 0.97 us
  other arithmetic: 1.39 us -> 0 us
    pallas_call x1, Pallas kernels: 70.3 us -> 60.1 us  [merge(): pl.pallas_call(functools.partial(kernel, nrow, n), out_shape=jax.ShapeDty...]
    unnamed x4 -> x1, local copies, waits for them, and re-layouts: 3.26 us -> 0.97 us
    slice x1 -> x0, local copies, waits for them, and re-layouts: 0.77 us -> none  [merge(): seam = jnp.stack([halves[0, rows - 1], halves[1, 0]]).astype(jnp.float32)]
where the time goes in v2:
time: 61.2 us; the launch traced here: 61.1 us
  Pallas kernels  60.1 us (98%)
  local copies, waits for them, and re-layouts  0.97 us (2%)
    pallas_call x1, Pallas kernels, merge(): pl.pallas_call(functools.partial(kernel, nrow, n), out_shape=jax.ShapeDty...  60.1 us

profile of v2, /device:TPU:1, one launch (start us, length us, event | category | flops | bytes accessed | tf_op | source)
XLA Modules:
  0.0 61.1 jit_solution(405172539631980780)
XLA Ops:
  0.0 60.1 %merge.1 = f32[2,512,256]{2,1,0:T(8,128)S(1)} custom-call(bf16[2,512,1024]{2,1,0:T(8,128)(2,1)} %halves.1, f32[8,2,128]{2,1,0:T(2,128)} %bitcast.5, s32[2,2,128]{2,1,0:T(2,128)} %bitcast.6, f32[2,2,128]{2,1,0:T(2,128)} %bitcast.7), custom_call_target="tpu_custom_call" | custom-call | tf_op jit(solution)/shard_map/merge/pallas_call | solution.py:372
  60.1 1.0 %copy.6 = f32[2,512,256]{2,1,0:T(8,128)} copy(f32[2,512,256]{2,1,0:T(8,128)S(1)} %merge.1) | data formatting | bytes 2097152

commit v3 on v2

--- a/solution.py
+++ b/solution.py
@@ -168,21 +168,43 @@
         pltpu.make_async_copy(ref, ref, sem).wait()
 
     near_copy.wait_recv()
+
+    def onward(o):
+        return copy_out(near, tab.at[0, z], tab_sem.at[6], tab_sem.at[2], (row, lax.rem(z + o, n), c))
+
+    @pl.when(c == 1)
+    def _():
+        for o in order:
+            onward(o).start()
+
     for a in range(2):
         spread(near[a], specb, a, other)
 
     others = pl.ds(0, n - 1)
     arrived(tab.at[c, others], tab_sem.at[1])
-    tab_swap = copy_out(tab.at[c], tab.at[c], tab_sem.at[2], tab_sem.at[3], (row, z, other))
-    tab_swap.start()
+    tab_swap = copy_out(tab.at[1], tab.at[1], tab_sem.at[3], tab_sem.at[2], (row, z, 0))
+
+    @pl.when(c == 1)
+    def _():
+        tab_swap.start()
+        tab[0, z] = near[...]
+
     pairs = [(dp, a) for dp in range(2) for a in range(2)]
     for dp, a in pairs:
         arrived(seam.at[dp, a], seam_recv.at[dp, a])
-    for dp, a in pairs:
-        spread(seam[dp, a], seamb, a, dp)
+    for dp in range(2):
+        spread(seam[dp, 0], seamb, 0, dp)
     arrived(want.at[others], want_sem.at[1])
     arrived(frac.at[others], frac_sem.at[1])
-    arrived(tab.at[other], tab_sem.at[3])
+
+    @pl.when(c == 0)
+    def _():
+        arrived(tab.at[1], tab_sem.at[2])
+
+    @pl.when(c == 1)
+    def _():
+        arrived(tab.at[0, others], tab_sem.at[2])
+
 
     table = (tab[...].reshape(4 * n * tiles, LANES) * 0.25).T
     hi = table.astype(jnp.bfloat16)
@@ -292,6 +314,11 @@
                 def _(way=way):
                     launch(jnp.minimum(i, 1), way, a)
 
+            @pl.when(jnp.logical_and(i == 0, a == 0))
+            def _():
+                for dp in range(2):
+                    spread(seam[dp, 1], seamb, 1, dp)
+
             return sums
 
         zeros = tuple(jnp.zeros((8, LANES), jnp.float32) for _ in range(kblocks))
@@ -322,7 +349,12 @@
     for ref, sem in ((tab.at[c, others], tab_sem), (want.at[others], want_sem), (frac.at[others], frac_sem)):
         arrived(ref, sem.at[0])
     arrived(ssq_s.at[others], ssq_sem.at[0])
-    tab_swap.wait_send()
+
+    @pl.when(c == 1)
+    def _():
+        tab_swap.wait_send()
+        arrived(tab.at[0, others], tab_sem.at[6])
+
     for d in a_swap:
         d.wait_send()
     near_copy.wait_send()
@@ -394,7 +426,7 @@
             pltpu.VMEM((n, kblocks, LANES), f32),
             pltpu.SemaphoreType.DMA((5,)),
             pltpu.SemaphoreType.DMA((6,)),
-            pltpu.SemaphoreType.DMA((6,)),
+            pltpu.SemaphoreType.DMA((7,)),
             pltpu.SemaphoreType.DMA((2,)),
             pltpu.SemaphoreType.DMA((2,)),
             pltpu.SemaphoreType.DMA,

time: 61.2 us -> 60.8 us (level)
  no operation moved by 1% of the time
where the time goes in v3:
time: 60.8 us
  Pallas kernels  59.8 us (98%)
  local copies, waits for them, and re-layouts  0.97 us (2%)
    pallas_call x1, Pallas kernels, merge(): pl.pallas_call(functools.partial(kernel, nrow, n), out_shape=jax.ShapeDty...  59.8 us

profile of v3, /device:TPU:1, one launch (start us, length us, event | category | flops | bytes accessed | tf_op | source)
XLA Modules:
  0.0 60.8 jit_solution(3754931509964642587)
XLA Ops:
  0.0 59.8 %merge.1 = f32[2,512,256]{2,1,0:T(8,128)S(1)} custom-call(bf16[2,512,1024]{2,1,0:T(8,128)(2,1)} %halves.1, f32[8,2,128]{2,1,0:T(2,128)} %bitcast.5, s32[2,2,128]{2,1,0:T(2,128)} %bitcast.6, f32[2,2,128]{2,1,0:T(2,128)} %bitcast.7), custom_call_target="tpu_custom_call" | custom-call | tf_op jit(solution)/shard_map/merge/pallas_call | solution.py:404
  59.8 1.0 %copy.6 = f32[2,512,256]{2,1,0:T(8,128)} copy(f32[2,512,256]{2,1,0:T(8,128)S(1)} %merge.1) | data formatting | bytes 2097152

commit v4 on v3

--- a/solution.py
+++ b/solution.py
@@ -35,6 +35,8 @@
     seamb,
     tcat,
     ct,
+    root,
+    ssq,
     part,
     sbuf,
     rbuf,
@@ -299,52 +301,82 @@
         sbuf[j, way, a] = total.astype(jnp.bfloat16)
         ring_copy(j, way, a).start()
 
-    def stage(i, carry):
-        odd = lax.rem(i, 2) == 1
-        off = jnp.where(odd, m - lax.div(i + 1, 2), lax.div(i, 2) - m)
+    def unit(u, carry):
+        ends = jnp.logical_or(u < 2, u >= 2 * n - 2)
+        pair = jnp.where(ends, jnp.where(u < 2, 0, m), lax.div(u + 2, 4))
+        turn = jnp.where(ends, 0, lax.rem(u, 2))
+        a = jnp.where(ends, lax.rem(u, 2), lax.div(lax.rem(u + 2, 4), 2))
+        off = jnp.where(turn == 0, m - pair, pair - m)
         slot = lax.rem(off + n, n)
-        lower, scaled = roots(at_offset(off))
-
-        def one(a, sums):
-            sums = cauchy(a, lower, scaled, sums)
-            product(slot, a)
+
+        @pl.when(a == 0)
+        def _():
+            lower, scaled = roots(at_offset(off))
+            root[turn, 0] = lower
+            root[turn, 1] = scaled
+            ssq[turn] = jnp.zeros(ssq.shape[1:], jnp.float32)
+
+        sums = cauchy(a, root[turn, 0], root[turn, 1], tuple(ssq[turn, b] for b in range(kblocks)))
+        product(slot, a)
+        for b in range(kblocks):
+            ssq[turn, b] = sums[b]
+
+        @pl.when(jnp.logical_and(c == 0, u == 2))
+        def _():
+            def both(k, carry):
+                for way in range(2):
+                    launch(0, way, k)
+                return carry
+
+            lax.fori_loop(0, 2, both, 0)
+
+        for way in range(2):
+            first = jnp.logical_or(
+                jnp.logical_and(u < 2, c == 1), jnp.logical_and(pair == 1, turn == way)
+            )
+
+            @pl.when(first)
+            def _(way=way):
+                launch(jnp.minimum(pair, 1), way, a)
+
+        @pl.when(u == 0)
+        def _():
+            for dp in range(2):
+                spread(seam[dp, 1], seamb, 1, dp)
+
+        @pl.when(a == 1)
+        def _():
+            for b in range(kblocks):
+                ssq_s[slot, b : b + 1, :] = jnp.sum(ssq[turn, b], axis=0, keepdims=True)
+
+            @pl.when(u < 2 * n - 1)
+            def _():
+                ssq_copy(off).start()
+
+        @pl.when(jnp.logical_and(lax.rem(u, 4) == 1, jnp.logical_and(u >= 5, u < 2 * n - 2)))
+        def _():
+            relays(lax.div(u + 3, 4))
+
+        return carry
+
+    def relays(j):
+        def each(a, carry):
             for way in range(2):
-
-                @pl.when(jnp.logical_or(i == 0, i == way + 1))
-                def _(way=way):
-                    launch(jnp.minimum(i, 1), way, a)
-
-            @pl.when(jnp.logical_and(i == 0, a == 0))
-            def _():
-                for dp in range(2):
-                    spread(seam[dp, 1], seamb, 1, dp)
-
-            return sums
-
-        zeros = tuple(jnp.zeros((8, LANES), jnp.float32) for _ in range(kblocks))
-        sums = lax.fori_loop(0, 2, one, zeros)
-        for b in range(kblocks):
-            ssq_s[slot, b : b + 1, :] = jnp.sum(sums[b], axis=0, keepdims=True)
-
-        @pl.when(i >= 3)
-        def _():
-            def each(a, carry):
-                for way in range(2):
-                    relay(i - 1, way, a)
-                return carry
-
-            lax.fori_loop(0, 2, each, 0)
-
-        @pl.when(i < n - 1)
-        def _():
-            ssq_copy(off).start()
-
-        return carry
+                relay(j, way, a)
+            return carry
+
+        lax.fori_loop(0, 2, each, 0)
 
     a_local.wait()
     for d in a_swap:
         d.wait_recv()
-    lax.fori_loop(0, n, stage, 0)
+    lax.fori_loop(0, 2 * n, unit, 0)
+
+    def rest(j, carry):
+        relays(j)
+        return carry
+
+    lax.fori_loop(m + 1, steps, rest, 0)
 
     for ref, sem in ((tab.at[c, others], tab_sem), (want.at[others], want_sem), (frac.at[others], frac_sem)):
         arrived(ref, sem.at[0])
@@ -419,6 +451,8 @@
             pltpu.VMEM((2, 2 * width, LANES), f32),
             pltpu.VMEM((3 * LANES, 4 * n * tiles), bf16),
             pltpu.VMEM((2 * width, cols), bf16),
+            pltpu.VMEM((2, 2, 1, cols), f32),
+            pltpu.VMEM((2, kblocks, 8, LANES), f32),
             pltpu.VMEM((n, 2, rows, cols), f32),
             pltpu.VMEM((steps, 2, 2, half, cols), bf16),
             pltpu.VMEM((steps, 2, 2, half, cols), bf16),

time: 60.8 us -> 59.6 us (0.980)
  Pallas kernels: 59.8 us -> 58.5 us
    pallas_call x1, Pallas kernels: 59.8 us -> 58.5 us  [merge(): pl.pallas_call(functools.partial(kernel, nrow, n), out_shape=jax.ShapeDty...]
where the time goes in v4:
time: 59.6 us; the launch traced here: 59.5 us
  Pallas kernels  58.5 us (98%)
  local copies, waits for them, and re-layouts  0.97 us (2%)
    pallas_call x1, Pallas kernels, merge(): pl.pallas_call(functools.partial(kernel, nrow, n), out_shape=jax.ShapeDty...  58.5 us

profile of v4, /device:TPU:1, one launch (start us, length us, event | category | flops | bytes accessed | tf_op | source)
XLA Modules:
  0.0 59.5 jit_solution(11194606833158348306)
XLA Ops:
  0.0 58.5 %merge.1 = f32[2,512,256]{2,1,0:T(8,128)S(1)} custom-call(bf16[2,512,1024]{2,1,0:T(8,128)(2,1)} %halves.1, f32[8,2,128]{2,1,0:T(2,128)} %bitcast.5, s32[2,2,128]{2,1,0:T(2,128)} %bitcast.6, f32[2,2,128]{2,1,0:T(2,128)} %bitcast.7), custom_call_target="tpu_custom_call" | custom-call | tf_op jit(solution)/shard_map/merge/pallas_call | solution.py:436
  58.5 1.0 %copy.6 = f32[2,512,256]{2,1,0:T(8,128)} copy(f32[2,512,256]{2,1,0:T(8,128)S(1)} %merge.1) | data formatting | bytes 2097152

commit v5 on v4

--- a/solution.py
+++ b/solution.py
@@ -139,7 +139,7 @@
             edge_row.at[a],
             seam.at[c, a],
             seam_send,
-            seam_recv.at[c, a],
+            seam_recv,
             (lax.rem(row + i, nrow), z, where_c),
         )
 
@@ -152,7 +152,7 @@
                 seam_copy(a, i, 1).start()
                 return carry
 
-            pltpu.make_async_copy(edge_row.at[a], seam.at[c, a], seam_recv.at[c, a]).start()
+            pltpu.make_async_copy(edge_row.at[a], seam.at[c, a], seam_recv).start()
             seam_copy(a, 0, other).start()
             lax.fori_loop(1, nrow, one, 0)
 
@@ -192,8 +192,7 @@
         tab[0, z] = near[...]
 
     pairs = [(dp, a) for dp in range(2) for a in range(2)]
-    for dp, a in pairs:
-        arrived(seam.at[dp, a], seam_recv.at[dp, a])
+    arrived(seam, seam_recv)
     for dp in range(2):
         spread(seam[dp, 0], seamb, 0, dp)
     arrived(want.at[others], want_sem.at[1])
@@ -280,8 +279,8 @@
         return copy_out(
             sbuf.at[j, way, a],
             rbuf.at[j, way, a],
-            ring_send.at[way, a],
-            ring_recv.at[j, way, a],
+            ring_send,
+            ring_recv.at[j, way],
             (row, lax.rem(z + step, n), c),
         )
 
@@ -296,7 +295,6 @@
         ring_copy(j, way, a).start()
 
     def relay(j, way, a):
-        ring_copy(j - 2, way, a).wait_recv()
         total = mine(j, way, a) + rbuf[j - 2, way, a].astype(jnp.float32)
         sbuf[j, way, a] = total.astype(jnp.bfloat16)
         ring_copy(j, way, a).start()
@@ -360,12 +358,14 @@
         return carry
 
     def relays(j):
-        def each(a, carry):
-            for way in range(2):
+        for way in range(2):
+            arrived(rbuf.at[j - 2, way], ring_recv.at[j - 2, way])
+
+            def each(a, carry, way=way):
                 relay(j, way, a)
-            return carry
-
-        lax.fori_loop(0, 2, each, 0)
+                return carry
+
+            lax.fori_loop(0, 2, each, 0)
 
     a_local.wait()
     for d in a_swap:
@@ -404,23 +404,19 @@
     norm = jnp.concatenate([norm[b : b + 1] for b in range(kblocks)], axis=1)
     inverse = 1.0 / norm
 
-    def landed(j, way, a):
-        ring_copy(j, way, a).wait_recv()
+    def landed(j, way):
+        arrived(rbuf.at[j, way], ring_recv.at[j, way])
         hh = (j + way) % 2
-        return slice(hh * half, (hh + 1) * half), rbuf[j, way, a].astype(jnp.float32)
-
-    for a in range(2):
-        for way in range(2):
-            at, value = landed(steps - 2, way, a)
-            part[0, a, at, :] += value
-    for a in range(2):
-        for way in range(2):
-            at, value = landed(steps - 1, way, a)
-            out[a, at, :] = (part[0, a, at, :] + value) * inverse
+        return slice(hh * half, (hh + 1) * half), rbuf[j, way].astype(jnp.float32)
 
     for way in range(2):
-        for a in range(2):
-            arrived(sbuf.at[:, way, a], ring_send.at[way, a])
+        at, value = landed(steps - 2, way)
+        part[0, :, at, :] += value
+    for way in range(2):
+        at, value = landed(steps - 1, way)
+        out[:, at, :] = (part[0, :, at, :] + value) * inverse
+
+    arrived(sbuf, ring_send)
 
 
 def merge(nrow, n, halves, spectrum, wanted, fraction):
@@ -464,9 +460,9 @@
             pltpu.SemaphoreType.DMA((2,)),
             pltpu.SemaphoreType.DMA((2,)),
             pltpu.SemaphoreType.DMA,
-            pltpu.SemaphoreType.DMA((2, 2)),
-            pltpu.SemaphoreType.DMA((2, 2)),
-            pltpu.SemaphoreType.DMA((steps, 2, 2)),
+            pltpu.SemaphoreType.DMA,
+            pltpu.SemaphoreType.DMA,
+            pltpu.SemaphoreType.DMA((steps, 2)),
             pltpu.SemaphoreType.DMA((2,)),
         ],
         compiler_params=pltpu.CompilerParams(

time: 59.6 us -> 59.4 us (level)
  no operation moved by 1% of the time
where the time goes in v5:
time: 59.4 us
  Pallas kernels  58.4 us (98%)
  local copies, waits for them, and re-layouts  0.97 us (2%)
    pallas_call x1, Pallas kernels, merge(): pl.pallas_call(functools.partial(kernel, nrow, n), out_shape=jax.ShapeDty...  58.4 us

profile of v5, /device:TPU:1, one launch (start us, length us, event | category | flops | bytes accessed | tf_op | source)
XLA Modules:
  0.0 59.4 jit_solution(571149116771232568)
XLA Ops:
  0.0 58.4 %merge.1 = f32[2,512,256]{2,1,0:T(8,128)S(1)} custom-call(bf16[2,512,1024]{2,1,0:T(8,128)(2,1)} %halves.1, f32[8,2,128]{2,1,0:T(2,128)} %bitcast.5, s32[2,2,128]{2,1,0:T(2,128)} %bitcast.6, f32[2,2,128]{2,1,0:T(2,128)} %bitcast.7), custom_call_target="tpu_custom_call" | custom-call | tf_op jit(solution)/shard_map/merge/pallas_call | solution.py:432
  58.4 1.0 %copy.6 = f32[2,512,256]{2,1,0:T(8,128)} copy(f32[2,512,256]{2,1,0:T(8,128)S(1)} %merge.1) | data formatting | bytes 2097152

commit v6 on v5

--- a/solution.py
+++ b/solution.py
@@ -319,14 +319,10 @@
         for b in range(kblocks):
             ssq[turn, b] = sums[b]
 
-        @pl.when(jnp.logical_and(c == 0, u == 2))
-        def _():
-            def both(k, carry):
-                for way in range(2):
-                    launch(0, way, k)
-                return carry
-
-            lax.fori_loop(0, 2, both, 0)
+        @pl.when(jnp.logical_and(c == 0, jnp.logical_or(u == 2, u == 3)))
+        def _():
+            for way in range(2):
+                launch(0, way, u - 2)
 
         for way in range(2):
             first = jnp.logical_or(

time: 59.4 us -> 59.1 us (level); the launches traced: 59.4 us -> 58.2 us
  Pallas kernels: 58.4 us -> 57.2 us
    pallas_call x1, Pallas kernels: 58.4 us -> 57.2 us  [merge(): pl.pallas_call(functools.partial(kernel, nrow, n), out_shape=jax.ShapeDty...]
where the time goes in v6:
time: 59.1 us; the launch traced here: 58.2 us
  Pallas kernels  57.2 us (97%)
  local copies, waits for them, and re-layouts  0.97 us (2%)
    pallas_call x1, Pallas kernels, merge(): pl.pallas_call(functools.partial(kernel, nrow, n), out_shape=jax.ShapeDty...  57.2 us

profile of v6, /device:TPU:1, one launch (start us, length us, event | category | flops | bytes accessed | tf_op | source)
XLA Modules:
  0.0 58.2 jit_solution(5211246956759832703)
XLA Ops:
  0.0 57.2 %merge.1 = f32[2,512,256]{2,1,0:T(8,128)S(1)} custom-call(bf16[2,512,1024]{2,1,0:T(8,128)(2,1)} %halves.1, f32[8,2,128]{2,1,0:T(2,128)} %bitcast.5, s32[2,2,128]{2,1,0:T(2,128)} %bitcast.6, f32[2,2,128]{2,1,0:T(2,128)} %bitcast.7), custom_call_target="tpu_custom_call" | custom-call | tf_op jit(solution)/shard_map/merge/pallas_call | solution.py:428
  57.2 1.0 %copy.6 = f32[2,512,256]{2,1,0:T(8,128)} copy(f32[2,512,256]{2,1,0:T(8,128)S(1)} %merge.1) | data formatting | bytes 2097152
